TPU v7x, 512 devices: a whole 4x8x8 slice. The times are simulated.
512 devices in a mesh: cell: 32 (over x, y), gene: 16 (over z, core).
Axes of the slice: x: 4, y: 8, z: 8, core: 2. Of those that a mesh axis runs over, the one named last changes fastest.
Arguments:
- counts: int32 [8192, 10240], P('cell', 'gene'), may hold values from 1 to 8
- cell_factors: float32 [64, 8192], P(None, 'cell'), may hold values from -6 to 6
- loadings: float32 [64, 10240], P(None, 'gene'), may hold values from -3 to 3
- cell_momenta: float32 [64, 8192], P(None, 'cell'), may hold values from -6 to 6
- loading_momenta: float32 [64, 10240], P(None, 'gene'), may hold values from -6 to 6
- step: float32 [64], replicated, may hold values from 0.01 to 0.04
Outputs:
- new_factors: float32 [64, 8192], P(None, 'cell')
- new_loadings: float32 [64, 10240], P(None, 'gene')
- new_cell_momenta: float32 [64, 8192], P(None, 'cell')
- new_loading_momenta: float32 [64, 10240], P(None, 'gene')
- log_rate: bfloat16 [8192, 10240], P('cell', 'gene')
All inputs are finite; a program needn't handle non-finite values.
Results may differ from a plain program's by a relative error of at most 0.001.
Values sent between devices are 32-bit elements; how exact they have to be, the bound alone decides.
A program may use at most 64 MiB of HBM per device.

v0:
```python
import jax
import jax.numpy as jnp
from jax import lax
from jax.sharding import PartitionSpec as P

K = 64


def from_everyone(array, axis):
    copies = jnp.broadcast_to(array, (lax.axis_size(axis), *array.shape))
    return lax.all_to_all(copies, axis, split_axis=0, concat_axis=0, tiled=True)


def of_everyone(array, axis):
    everything = from_everyone(array, axis)
    return jnp.sum(everything, axis=0)


def together(arrays, axis):
    flat, at, outs = (jnp.concatenate([a.reshape(-1) for a in arrays]), 0, [])
    so_far = of_everyone(flat, axis)
    for a in arrays:
        outs.append(so_far[at : at + a.size].reshape(a.shape))
        at += a.size
    return tuple(outs)


def over_pieces(array, axis):
    parts = lax.all_gather(array, axis)
    return parts.sum(axis=0)


def in_blocks(array, dim, peers):
    dims = array.shape
    parts = array.reshape(*dims[:dim], peers, dims[dim] // peers, *dims[dim + 1 :])
    return jnp.moveaxis(parts, dim, 0)


def summed_on_arrival(array, axis, dim):
    parts = in_blocks(array, dim, lax.axis_size(axis))
    arrived = lax.all_to_all(parts, axis, split_axis=0, concat_axis=0, tiled=True)
    return arrived.sum(axis=0)


def in_order(parts, dim):
    parts = jnp.moveaxis(parts, 0, dim)
    dims = parts.shape
    return parts.reshape(*dims[:dim], dims[dim] * dims[dim + 1], *dims[dim + 2 :])


def gather_directly(array, axis, dim):
    return in_order(from_everyone(array, axis), dim)


def local(counts, cell_factors, loadings, cell_momenta, loading_momenta, step):
    scale = 1.0 / jnp.sqrt(jnp.float32(K))
    counts_float = counts.astype(jnp.float32)
    library = of_everyone(jnp.sum(counts_float, axis=1), "gene")
    genes_total = jnp.float32(loadings.shape[1] * lax.axis_size("gene"))
    half = 0.5 * step[:, None]
    full = step[:, None]
    width = loadings.shape[1] // lax.axis_size("cell")
    offset = lax.axis_index("cell") * width

    def gradient(factors, loads, own_loads):
        linear = (
            lax.dot_general(
                factors, loads, (((0,), (0,)), ((), ())), precision=lax.Precision.HIGHEST
            )
            * scale
        )
        expo = jnp.exp(linear)
        squares = jnp.sum(loads * loads, axis=1)
        total, squares = together((jnp.sum(expo, axis=1), squares), "gene")
        size = library / total
        resid = counts_float - size[:, None] * expo
        cross = (
            lax.dot_general(loads, resid, (((1,), (1,)), ((), ())), precision=lax.Precision.HIGHEST)
            * scale
        )
        grad_u = over_pieces(cross, "gene") - factors
        ard = (genes_total + 2.0) / (squares + 2.0)
        part_v = jnp.dot(factors, resid, precision=lax.Precision.HIGHEST) * scale
        grad_v = summed_on_arrival(part_v, "cell", 1) - ard[:, None] * own_loads
        return (grad_u, grad_v, linear, size)

    factors = cell_factors
    mom_u = cell_momenta
    loads = loadings
    own = lax.dynamic_slice_in_dim(loadings, offset, width, 1)
    mom_v = lax.dynamic_slice_in_dim(loading_momenta, offset, width, 1)
    grad_u, grad_v, linear, size = gradient(factors, loads, own)
    mom_u = mom_u + half * grad_u
    mom_v = mom_v + half * grad_v
    factors = factors + full * mom_u
    own = own + full * mom_v
    loads = gather_directly(own, "cell", 1)
    grad_u, grad_v, linear, size = gradient(factors, loads, own)
    mom_u = mom_u + half * grad_u
    mom_v = mom_v + half * grad_v
    mom_v = gather_directly(mom_v, "cell", 1)
    rates = (linear + jnp.log(size)[:, None]).astype(jnp.bfloat16)
    return (factors, loads, mom_u, mom_v, rates)


def solution(mesh):
    placed = (
        P("cell", "gene"),
        P(None, "cell"),
        P(None, "gene"),
        P(None, "cell"),
        P(None, "gene"),
        P(),
    )
    return jax.shard_map(
        local,
        mesh=mesh,
        in_specs=placed,
        out_specs=(
            P(None, "cell"),
            P(None, "gene"),
            P(None, "cell"),
            P(None, "gene"),
            P("cell", "gene"),
        ),
        check_vma=False,
    )
```

profile of v0, /device:TPU:1, one launch (start us, length us, event | category | flops | bytes accessed | tf_op | source)
XLA Modules:
  0.0 143.3 jit_solution(7986956964208528517)
XLA Ops:
  7.2 0.0 copy-start
  7.2 0.0 copy-start.2
  7.2 1.3 convert_reduce_fusion
  8.5 0.6 broadcast_in_dim.10
  9.1 12.0 %all-to-all-start = ((f32[16,1,256]{2,1,0:T(1,128)}), f32[16,1,256]{2,1,0:T(1,128)S(1)}, u32[]{:S(2)}, u32[]{:S(2)}) async-start(f32[16,1,256]{2,1,0:T(1,128)} %broadcast_in_dim.10), calls=%async_computation | async-start | bytes 32768 | tf_op jit(solution)/shard_map/all_to_all | solution.py:11
  21.0 0.0 copy-done.6
  21.0 0.0 copy-start.1
  21.1 0.0 copy-done.2
  21.1 0.1 multiply_reduce_fusion.1
  21.2 0.0 copy-done.4
  21.2 0.9 fusion.4
  22.1 6.3 %all-to-all-done = f32[16,1,256]{2,1,0:T(1,128)S(1)} async-done(((f32[16,1,256]{2,1,0:T(1,128)}), f32[16,1,256]{2,1,0:T(1,128)S(1)}, u32[]{:S(2)}, u32[]{:S(2)}) %all-to-all-start) | async-done | bytes 16416 | tf_op jit(solution)/shard_map/all_to_all | solution.py:11
  28.4 0.6 broadcast_in_dim.11
  29.0 3.7 %all-to-all-start.1 = ((f32[16,1,320]{2,1,0:T(1,128)}), f32[16,1,320]{2,1,0:T(1,128)S(1)}, u32[]{:S(2)}, u32[]{:S(2)}) async-start(f32[16,1,320]{2,1,0:T(1,128)} %broadcast_in_dim.11), calls=%async_computation.1 | async-start | bytes 49152 | tf_op jit(solution)/shard_map/all_to_all | solution.py:11
  32.7 0.0 all-gather.5.cloned.1.call-start
  32.7 0.0 copy-done
  32.7 0.1 constant_dynamic-slice_fusion
  32.8 0.1 copy.43
  32.9 7.2 %all-to-all-done.1 = f32[16,1,320]{2,1,0:T(1,128)S(1)} async-done(((f32[16,1,320]{2,1,0:T(1,128)}), f32[16,1,320]{2,1,0:T(1,128)S(1)}, u32[]{:S(2)}, u32[]{:S(2)}) %all-to-all-start.1) | async-done | bytes 20512 | tf_op jit(solution)/shard_map/all_to_all | solution.py:11
  40.2 0.0 copy-done.1
  40.2 1.5 %fusion.2 = f32[64,256]{1,0:T(8,128)} fusion(f32[64,640]{1,0:T(8,128)S(1)} %copy-done.2, f32[256,640]{1,0:T(8,128)S(1)} %get-tuple-element.28, s32[256,640]{1,0:T(8,128)S(1)} %copy-done.1, f32[256]{0:T(256)S(1)} %slice_divide_fusion.1), kind=kOutput, calls=%fused_computation.8 | convolution fusion | flops 126337024 | bytes 1541120 | tf_op jit(solution)/shard_map/dot_general | solution.py:78
  41.7 0.0 all-gather.5.cloned.1.call-update
  41.7 0.6 fusion.1
  42.4 0.2 copy.33
  42.6 0.9 reshape.48
  43.5 9.7 %all-to-all-start.2 = ((f32[32,1,1280]{2,1,0:T(1,128)}), f32[32,1,1280]{2,1,0:T(1,128)S(1)}, u32[]{:S(2)}, u32[]{:S(2)}) async-start(f32[32,1,1280]{2,1,0:T(1,128)} %reshape.48), calls=%async_computation.2 | async-start | bytes 327680 | tf_op jit(solution)/shard_map/all_to_all | solution.py:41
  53.2 0.0 all-gather.7.cloned.1.call-start
  53.2 0.1 constant_dynamic-slice_fusion.1
  53.3 0.1 copy.42
  53.4 9.0 %all-to-all-done.2 = f32[32,1,1280]{2,1,0:T(1,128)S(1)} async-done(((f32[32,1,1280]{2,1,0:T(1,128)}), f32[32,1,1280]{2,1,0:T(1,128)S(1)}, u32[]{:S(2)}, u32[]{:S(2)}) %all-to-all-start.2) | async-done | bytes 163872 | tf_op jit(solution)/shard_map/all_to_all | solution.py:41
  62.4 0.6 broadcast.57
  63.0 1.1 reduce.4
  64.1 0.1 reshape.49
  64.3 0.2 reshape.50
  64.5 14.0 %all_to_all.38 = f32[32,1,1280]{2,1,0:T(1,128)S(1)} all-to-all(f32[32,1,1280]{2,1,0:T(1,128)S(1)} %reshape.50), channel_id=1, replica_groups=mesh['cell'=32,'gene'=16] {'cell'}, dimensions={0} | all-to-all | bytes 327680 | tf_op jit(solution)/shard_map/all_to_all | solution.py:11
  78.5 1.1 reduce.5
  79.6 0.1 reshape.51
  79.8 0.1 multiply_reduce_fusion
  79.9 0.3 all-gather.5.cloned.1.call-done
  80.2 1.3 reduce_sum.113
  81.5 0.0 copy-done.5
  81.6 0.1 multiply_add_fusion.1
  81.6 0.0 copy-start.3
  81.7 1.0 exponential_reduce_fusion
  82.7 12.4 %all_to_all.39 = f32[16,1,320]{2,1,0:T(1,128)S(1)} all-to-all(f32[16,1,320]{2,1,0:T(1,128)S(1)} %broadcast_in_dim.25), channel_id=1, replica_groups=mesh['cell'=32,'gene'=16] {'gene'}, dimensions={0} | all-to-all | bytes 40960 | tf_op jit(solution)/shard_map/all_to_all | solution.py:11
  95.2 1.5 %convolution_multiply_fusion.4 = f32[64,256]{1,0:T(8,128)} fusion(f32[64,640]{0,1:T(8,128)S(1)} %reshape.43, s32[256,640]{1,0:T(8,128)S(1)} %copy-done.1, f32[256,640]{1,0:T(8,128)S(1)} %get-tuple-element.30, f32[256]{0:T(256)S(1)} %get-tuple-element.26), kind=kOutput, calls=%fused_computation.6 | convolution fusion | flops 126337024 | bytes 1541120 | tf_op jit(solution)/shard_map/dot_general | solution.py:78
  96.6 0.0 all-gather.7.cloned.1.call-update
  96.7 0.6 convolution_multiply_fusion.2
  97.3 0.2 copy.35
  97.5 0.9 reshape.52
  98.4 8.3 %all-to-all-start.5 = ((f32[32,1,1280]{2,1,0:T(1,128)}), f32[32,1,1280]{2,1,0:T(1,128)S(1)}, u32[]{:S(2)}, u32[]{:S(2)}) async-start(f32[32,1,1280]{2,1,0:T(1,128)} %reshape.52), calls=%async_computation.5 | async-start | bytes 327680 | tf_op jit(solution)/shard_map/all_to_all | solution.py:41
  106.8 9.2 %all-to-all-done.5 = f32[32,1,1280]{2,1,0:T(1,128)S(1)} async-done(((f32[32,1,1280]{2,1,0:T(1,128)}), f32[32,1,1280]{2,1,0:T(1,128)S(1)}, u32[]{:S(2)}, u32[]{:S(2)}) %all-to-all-start.5) | async-done | bytes 163872 | tf_op jit(solution)/shard_map/all_to_all | solution.py:41
  116.0 1.1 reduce.6
  117.1 0.1 reshape.53
  117.3 0.9 reshape.54
  118.2 4.9 %all-to-all-start.6 = ((f32[32,1,1280]{2,1,0:T(1,128)}), f32[32,1,1280]{2,1,0:T(1,128)S(1)}, u32[]{:S(2)}, u32[]{:S(2)}) async-start(f32[32,1,1280]{2,1,0:T(1,128)} %reshape.54), calls=%async_computation.6 | async-start | bytes 327680 | tf_op jit(solution)/shard_map/all_to_all | solution.py:11
  123.1 0.8 copy.36
  123.9 0.8 add_convert_fusion
  124.8 7.6 %all-to-all-done.6 = f32[32,1,1280]{2,1,0:T(1,128)S(1)} async-done(((f32[32,1,1280]{2,1,0:T(1,128)}), f32[32,1,1280]{2,1,0:T(1,128)S(1)}, u32[]{:S(2)}, u32[]{:S(2)}) %all-to-all-start.6) | async-done | bytes 163872 | tf_op jit(solution)/shard_map/all_to_all | solution.py:11
  132.4 1.1 reduce.7
  133.4 0.1 reshape.55
  133.6 0.8 copy.37
  134.5 1.3 reduce_sum.118
  135.8 0.7 multiply_add_fusion
  (30 shorter events, 0.6 us)
Async XLA Ops:
  7.2 25.6 %copy-start = (f32[64,640]{1,0:T(8,128)S(1)}, f32[64,640]{1,0:T(8,128)}, u32[]{:S(2)}) copy-start(f32[64,640]{1,0:T(8,128)} %param.10) | copy-start | bytes 491524
  7.2 13.9 %copy-start.2 = (f32[64,640]{1,0:T(8,128)S(1)}, f32[64,640]{1,0:T(8,128)}, u32[]{:S(2)}) copy-start(f32[64,640]{1,0:T(8,128)} %param.8) | copy-start | bytes 491524
  8.5 12.6 %copy-start.6 = (f32[64]{0:T(128)S(1)}, f32[64]{0:T(128)}, u32[]{:S(2)}) copy-start(f32[64]{0:T(128)} %param.11) | copy-start | bytes 772
  9.1 12.1 %copy-start.4 = (f32[64,256]{1,0:T(8,128)S(1)}, f32[64,256]{1,0:T(8,128)}, u32[]{:S(2)}) copy-start(f32[64,256]{1,0:T(8,128)} %param.7) | copy-start | bytes 196612
  9.1 19.3 %all-to-all-start = ((f32[16,1,256]{2,1,0:T(1,128)}), f32[16,1,256]{2,1,0:T(1,128)S(1)}, u32[]{:S(2)}, u32[]{:S(2)}) async-start(f32[16,1,256]{2,1,0:T(1,128)} %broadcast_in_dim.10), calls=%async_computation | async-start | bytes 32768 | tf_op jit(solution)/shard_map/all_to_all | solution.py:11
  21.0 19.2 %copy-start.1 = (s32[256,640]{1,0:T(8,128)S(1)}, s32[256,640]{1,0:T(8,128)}, u32[]{:S(2)}) copy-start(s32[256,640]{1,0:T(8,128)} %param.6) | copy-start | bytes 1966084
  29.0 11.2 %all-to-all-start.1 = ((f32[16,1,320]{2,1,0:T(1,128)}), f32[16,1,320]{2,1,0:T(1,128)S(1)}, u32[]{:S(2)}, u32[]{:S(2)}) async-start(f32[16,1,320]{2,1,0:T(1,128)} %broadcast_in_dim.11), calls=%async_computation.1 | async-start | bytes 49152 | tf_op jit(solution)/shard_map/all_to_all | solution.py:11
  32.7 47.5 %all-gather.5.cloned.1.call-start = ((), (), s32[]{:S(2)}) async-start(), calls=%async_computation.7 | async-start | bytes 1114112 | tf_op jit(solution)/shard_map/all_gather | solution.py:29
  43.5 18.9 %all-to-all-start.2 = ((f32[32,1,1280]{2,1,0:T(1,128)}), f32[32,1,1280]{2,1,0:T(1,128)S(1)}, u32[]{:S(2)}, u32[]{:S(2)}) async-start(f32[32,1,1280]{2,1,0:T(1,128)} %reshape.48), calls=%async_computation.2 | async-start | bytes 327680 | tf_op jit(solution)/shard_map/all_to_all | solution.py:41
  53.2 81.3 %all-gather.7.cloned.1.call-start = ((), (), s32[]{:S(2)}) async-start(), calls=%async_computation.8 | async-start | bytes 1114112 | tf_op jit(solution)/shard_map/all_gather | solution.py:29
  80.2 1.3 copy-start.5
  81.6 54.1 %copy-start.3 = (f32[64,256]{1,0:T(8,128)}, f32[64,256]{1,0:T(8,128)S(1)}, u32[]{:S(2)}) copy-start(f32[64,256]{1,0:T(8,128)S(1)} %multiply_add_fusion.1) | copy-start | bytes 196612
  98.4 17.6 %all-to-all-start.5 = ((f32[32,1,1280]{2,1,0:T(1,128)}), f32[32,1,1280]{2,1,0:T(1,128)S(1)}, u32[]{:S(2)}, u32[]{:S(2)}) async-start(f32[32,1,1280]{2,1,0:T(1,128)} %reshape.52), calls=%async_computation.5 | async-start | bytes 327680 | tf_op jit(solution)/shard_map/all_to_all | solution.py:41
  118.2 14.2 %all-to-all-start.6 = ((f32[32,1,1280]{2,1,0:T(1,128)}), f32[32,1,1280]{2,1,0:T(1,128)S(1)}, u32[]{:S(2)}, u32[]{:S(2)}) async-start(f32[32,1,1280]{2,1,0:T(1,128)} %reshape.54), calls=%async_computation.6 | async-start | bytes 327680 | tf_op jit(solution)/shard_map/all_to_all | solution.py:11
Sparse Core Ops, SparseCore 0:
  41.8 38.3 all-gather.4
  96.8 37.0 all-gather.6
where the time goes:
time: 145 us; the launch traced here: 143 us
  waiting for transfers between devices  39.8 us (27%)
  starting transfers between devices  38.6 us (27%)
  blocking collectives  26.4 us (18%)
  between operations  14.4 us (10%)
  other arithmetic  10.3 us (7%)
  local copies, waits for them, and re-layouts  7.73 us (5%)
  matrix products  6.04 us (4%)
    all_to_all x2, blocking collectives, from_everyone(): return lax.all_to_all(copies, axis, split_axis=0, concat_axis=0, tiled=True)  26.4 us
    all_to_all x3, waiting for transfers between devices, from_everyone(): return lax.all_to_all(copies, axis, split_axis=0, concat_axis=0, tiled=True)  21.1 us
    all_to_all x3, starting transfers between devices, from_everyone(): return lax.all_to_all(copies, axis, split_axis=0, concat_axis=0, tiled=True)  20.6 us
    all_to_all x2, waiting for transfers between devices, summed_on_arrival(): lax.all_to_all(parts, axis, split_axis=0, concat_axis=0, tiled=True)  18.3 us
    all_to_all x2, starting transfers between devices, summed_on_arrival(): lax.all_to_all(parts, axis, split_axis=0, concat_axis=0, tiled=True)  18 us
    unnamed x30, local copies, waits for them, and re-layouts  5.22 us
    dot_general x2, matrix products, gradient(): lax.dot_general(loads, resid, (((1,), (1,)), ((), ())), precision=lax.Pre...  2.98 us
  transfers between devices with their start and end apart: 7, of which 6 were waited for; matrix products, arithmetic and copies ran while one was open for 10% of the time, Pallas kernels for 0%

commit v1 on v0

v1 whole, which is shorter than its diff:
```python
import jax
import jax.numpy as jnp
from jax import lax
from jax.experimental import pallas as pl
from jax.experimental.pallas import tpu as pltpu
from jax.sharding import PartitionSpec as P

K = 64
CELLS = 256
GENES = 640
XS = 4
YS = 8
ZS = 8
CORES = 2
LANES = 128
N_CELL = XS * YS
N_GENE = ZS * CORES
V_TILES = (K // 8) * (GENES // LANES)
U_TILES = (K // 8) * (CELLS // LANES)
EXTRA = V_TILES - N_CELL
COLS = GENES // LANES
UCOLS = CELLS // LANES
MESH = pl.DeviceIdType.MESH
F32 = jnp.float32
BF16 = jnp.bfloat16


def div(a, b):
    return lax.div(a, jnp.int32(b))


def rem(a, b):
    return lax.rem(a, jnp.int32(b))


def split(x):
    high = x.astype(BF16)
    return high, (x - high.astype(F32)).astype(BF16)


def zigzag(i, n):
    sign = 1 - 2 * rem(i, 2)
    return n // 2 + sign * div(i + 1, 2)


def tiles_sum(x):
    total = x[:, 0:LANES]
    for t in range(1, x.shape[1] // LANES):
        total = total + x[:, t * LANES : (t + 1) * LANES]
    return total


def row_of(part):
    return jnp.sum(part.T, axis=0, keepdims=True)


def col_of(row, block):
    lanes = lax.broadcasted_iota(jnp.int32, (8, LANES), 1)
    wanted = lax.broadcasted_iota(jnp.int32, (8, LANES), 0) + 8 * block
    return jnp.sum(jnp.where(lanes == wanted, jnp.broadcast_to(row, (8, LANES)), 0.0), axis=1, keepdims=True)


def kernel(
    counts_h, u_h, v_h, p_h, q_h, step_h,
    u_o, v_o, p_o, q_o, rate_o,
    cnt, u0, v0, p0, q0, stp,
    y16, lin, eh, el, part, lib, amat, cmat,
    r_tot, r_ls, r_sq, pu, r_ux, r_ua, r_mu, pv, r_vx, r_ve, r_va, r_mv, mv_keep, mu_keep,
    u1, v1, pfin, qfin, rate_v,
    in_sem, out_sem, send_sem, recv_sem, row_sem,
):
    cell = lax.axis_index("cell")
    gene = lax.axis_index("gene")
    cx, cy = div(cell, YS), rem(cell, YS)
    gz, gc = div(gene, CORES), rem(gene, CORES)
    owns_extra = rem(cy, XS) == cx

    loads = {}
    for n, (src, dst) in enumerate(((u_h, u0), (v_h, v0), (counts_h, cnt), (q_h, q0), (step_h, stp), (p_h, p0))):
        loads[n] = pltpu.make_async_copy(src, dst, in_sem.at[n])
        loads[n].start()

    def gene_peer(s):
        i = div(s, 2)
        zz = rem(gz + zigzag(i, ZS), ZS)
        cc = rem(gc + 1 - rem(s, 2), CORES)
        return zz * CORES + cc

    def cell_peer(s):
        xx = rem(cx + zigzag(rem(s, XS), XS), XS)
        yy = rem(cy + zigzag(div(s, XS), YS), YS)
        return xx * YS + yy

    barrier = pltpu.get_barrier_semaphore()

    def greet_gene(s, c):
        pl.semaphore_signal(barrier, inc=1, device_id={"gene": gene_peer(s)}, device_id_type=MESH)
        return c

    def greet_y(s, c):
        yy = rem(cy + s, YS)
        pl.semaphore_signal(barrier, inc=1, device_id={"cell": cx * YS + yy}, device_id_type=MESH)
        return c

    def greet_x(s, c):
        xx = rem(cx + s, XS)
        pl.semaphore_signal(barrier, inc=1, device_id={"cell": xx * YS + cy}, device_id_type=MESH)
        return c

    lax.fori_loop(0, N_GENE - 1, greet_gene, 0)
    lax.fori_loop(1, YS, greet_y, 0)
    lax.fori_loop(1, XS, greet_x, 0)

    def wait_bytes(ref, sem):
        pltpu.make_async_copy(ref, ref, sem).wait()

    def push(src, dst, phase, where):
        pltpu.make_async_remote_copy(
            src_ref=src, dst_ref=dst, send_sem=send_sem.at[phase], recv_sem=recv_sem.at[phase],
            device_id=where, device_id_type=MESH,
        ).start()

    def to_genes(src_of, dst, phase):
        def body(s, c):
            peer = gene_peer(s)
            push(src_of(peer), dst, phase, {"gene": peer})
            return c
        lax.fori_loop(0, N_GENE - 1, body, 0)

    def scatter_loadings(g, phase):
        def body(s, c):
            peer = cell_peer(s)
            push(pv.at[g, peer], r_vx.at[g, cell], phase, {"cell": peer})
            px, py = div(peer, YS), rem(peer, YS)

            @pl.when(rem(py, XS) == px)
            def _():
                push(pv.at[g, N_CELL + py], r_ve.at[g, cell], phase + 1, {"cell": peer})
            return c
        lax.fori_loop(0, N_CELL - 1, body, 0)

    def gather_loadings(buf, phase):
        def body(s, c):
            peer = cell_peer(s)
            push(buf.at[cell], buf.at[cell], phase, {"cell": peer})

            @pl.when(owns_extra)
            def _():
                push(buf.at[N_CELL + cy], buf.at[N_CELL + cy], phase + 1, {"cell": peer})
            return c
        lax.fori_loop(0, N_CELL - 1, body, 0)

    def scatter_sent(g, phase):
        wait_bytes(r_vx.at[g, pl.ds(0, N_CELL - 1)], send_sem.at[phase])

        @pl.when(owns_extra)
        def _():
            wait_bytes(r_vx.at[g, pl.ds(0, EXTRA - 1)], send_sem.at[phase + 1])

        @pl.when(jnp.logical_not(owns_extra))
        def _():
            wait_bytes(r_vx.at[g, pl.ds(0, EXTRA)], send_sem.at[phase + 1])

    def gather_sent(buf, phase):
        wait_bytes(buf.at[pl.ds(0, N_CELL - 1)], send_sem.at[phase])

        @pl.when(owns_extra)
        def _():
            wait_bytes(buf.at[pl.ds(0, N_CELL - 1)], send_sem.at[phase + 1])

    def gather_arrived(buf, phase):
        wait_bytes(buf.at[pl.ds(0, N_CELL - 1)], recv_sem.at[phase])

        @pl.when(owns_extra)
        def _():
            wait_bytes(buf.at[pl.ds(0, EXTRA - 1)], recv_sem.at[phase + 1])

        @pl.when(jnp.logical_not(owns_extra))
        def _():
            wait_bytes(buf.at[pl.ds(0, EXTRA)], recv_sem.at[phase + 1])

    chunks = []
    at = 0
    while at < GENES:
        chunks.append((at, min(256, GENES - at)))
        at += 256

    def exponentials(u, v):
        uh, ul = split(u * 0.125)
        uh32, ul32 = uh.astype(F32), ul.astype(F32)
        left = jnp.concatenate([uh32, uh32, ul32, ul32], axis=0).T.astype(BF16)
        vh, vl = split(v)
        right = jnp.concatenate([vh, vl, vh, vl], axis=0)
        for n, (lo, wide) in enumerate(chunks):
            x = jnp.dot(left, right[:, lo : lo + wide], preferred_element_type=F32)
            e = jnp.exp(x)
            lin[:, lo : lo + wide] = x
            high, low = split(e)
            eh[:, lo : lo + wide] = high
            el[:, lo : lo + wide] = low
            some = tiles_sum(e)
            part[...] = some if n == 0 else part[...] + some
        return row_of(part[...])

    def square_row(v):
        s = tiles_sum(v * v)
        return row_of(jnp.concatenate([s, jnp.zeros_like(s)], axis=0))

    def stacked(x):
        high, low = split(x)
        return jnp.concatenate([high, low], axis=0), high

    def across(both):
        return both[:K] + both[K:]

    over_genes = (((1,), (1,)), ((), ()))

    def counts_by_genes(v):
        pair, _ = stacked(v * 0.125)
        amat[...] = across(lax.dot_general(pair, y16[...], over_genes, preferred_element_type=F32))

    def expo_by_genes(v):
        pair, high = stacked(v * 0.125)
        both = lax.dot_general(pair, eh[...], over_genes, preferred_element_type=F32)
        rest = lax.dot_general(high, el[...], over_genes, preferred_element_type=F32)
        return across(both) + rest

    def counts_by_cells(u):
        pair, _ = stacked(u * 0.125)
        for lo, wide in chunks:
            cmat[:, lo : lo + wide] = across(jnp.dot(pair, y16[:, lo : lo + wide], preferred_element_type=F32))

    def loadings_parts(g, u, size):
        pair, high = stacked(u * (size * 0.125))
        for lo, wide in chunks:
            both = jnp.dot(pair, eh[:, lo : lo + wide], preferred_element_type=F32)
            rest = jnp.dot(high, el[:, lo : lo + wide], preferred_element_type=F32)
            piece = cmat[:, lo : lo + wide] - (across(both) + rest)
            for t in range(wide // LANES):
                for b in range(K // 8):
                    pv[g, b * COLS + lo // LANES + t] = piece[8 * b : 8 * b + 8, t * LANES : (t + 1) * LANES]

    def factor_parts(g, bmat, size):
        cross = amat[...] - size * bmat
        for b in range(K // 8):
            for t in range(UCOLS):
                pu[g, b * UCOLS + t] = cross[8 * b : 8 * b + 8, t * LANES : (t + 1) * LANES]

    def step_col(block):
        return col_of(stp[...], block)

    loads[0].wait()
    loads[1].wait()
    tot = exponentials(u0[...], v0[...])
    loads[2].wait()
    yf = cnt[...].astype(F32)
    y16[...] = yf.astype(BF16)
    part[...] = tiles_sum(yf)
    lib_own = row_of(part[...])
    r_tot[0, gene] = tot
    r_ls[gene] = jnp.concatenate([lib_own, square_row(v0[...])], axis=1)

    pl.semaphore_wait(barrier, (N_GENE - 1) + (YS - 1) + (XS - 1))

    to_genes(lambda peer: r_tot.at[0, gene], r_tot.at[0, gene], 0)
    to_genes(lambda peer: r_ls.at[gene], r_ls.at[gene], 1)

    def tell_x(s, c):
        xx = rem(cx + s, XS)
        pl.semaphore_signal(row_sem, inc=1, device_id={"cell": xx * YS + cy}, device_id_type=MESH)
        return c

    lax.fori_loop(1, XS, tell_x, 0)

    counts_by_cells(u0[...])
    counts_by_genes(v0[...])
    bmat = expo_by_genes(v0[...])
    for n in (3, 4, 5):
        loads[n].wait()

    wait_bytes(r_tot.at[0, pl.ds(0, N_GENE - 1)], recv_sem.at[0])
    wait_bytes(r_ls.at[pl.ds(0, N_GENE - 1)], recv_sem.at[1])
    both = jnp.sum(r_ls[...], axis=0)
    lib[...] = both[:, :CELLS]
    squares = both[:, CELLS:]
    size = lib[...] / jnp.sum(r_tot[0], axis=0)
    loadings_parts(0, u0[...], size)
    pl.semaphore_wait(row_sem, XS - 1)
    scatter_loadings(0, 2)
    r_vx[0, cell] = pv[0, cell]

    factor_parts(0, bmat, size)
    to_genes(lambda peer: pu.at[0, peer], r_ux.at[0, gene], 4)
    r_ux[0, gene] = pu[0, gene]

    ub, ut = div(gene, UCOLS), rem(gene, UCOLS)
    urow, ucol = pl.multiple_of(ub * 8, 8), pl.multiple_of(ut * LANES, LANES)
    ustep = step_col(ub)
    u_tile = u0[pl.ds(urow, 8), pl.ds(ucol, LANES)]
    p_tile = p0[pl.ds(urow, 8), pl.ds(ucol, LANES)]
    wait_bytes(r_ux.at[0, pl.ds(0, N_GENE - 1)], recv_sem.at[4])
    grad = jnp.sum(r_ux[0], axis=0) - u_tile
    p_tile = p_tile + 0.5 * ustep * grad
    mu_keep[...] = p_tile
    r_ua[gene] = u_tile + ustep * p_tile
    to_genes(lambda peer: r_ua.at[gene], r_ua.at[gene], 5)

    def v_tile_of(tile):
        b, t = div(tile, COLS), rem(tile, COLS)
        row, col = pl.multiple_of(b * 8, 8), pl.multiple_of(t * LANES, LANES)
        return b, (pl.ds(row, 8), pl.ds(col, LANES))

    genes_total = float(GENES * N_GENE) + 2.0

    def first_update(tile, arrived, keep):
        b, where = v_tile_of(tile)
        vs = step_col(b)
        ard = genes_total / (col_of(squares, b) + 2.0)
        v = v0[where]
        mom = q0[where] + 0.5 * vs * (jnp.sum(arrived, axis=0) - ard * v)
        mv_keep[keep] = mom
        r_va[tile] = v + vs * mom

    def arrived_parts(g, phase):
        wait_bytes(r_vx.at[g, pl.ds(0, N_CELL - 1)], recv_sem.at[phase])

        @pl.when(owns_extra)
        def _():
            r_ve[g, cell] = pv[g, N_CELL + cy]
            wait_bytes(r_ve.at[g, pl.ds(0, N_CELL - 1)], recv_sem.at[phase + 1])

    arrived_parts(0, 2)
    first_update(cell, r_vx[0], 0)

    @pl.when(owns_extra)
    def _():
        first_update(N_CELL + cy, r_ve[0], 1)

    gather_loadings(r_va, 6)

    wait_bytes(r_ua.at[pl.ds(0, N_GENE - 1)], recv_sem.at[5])
    for b in range(K // 8):
        for t in range(UCOLS):
            u1[8 * b : 8 * b + 8, t * LANES : (t + 1) * LANES] = r_ua[b * UCOLS + t]
    out_u = pltpu.make_async_copy(u1, u_o, out_sem.at[0])
    out_u.start()
    counts_by_cells(u1[...])

    gather_arrived(r_va, 6)
    for b in range(K // 8):
        for t in range(COLS):
            v1[8 * b : 8 * b + 8, t * LANES : (t + 1) * LANES] = r_va[b * COLS + t]
    out_v = pltpu.make_async_copy(v1, v_o, out_sem.at[1])
    out_v.start()

    r_tot[1, gene] = exponentials(u1[...], v1[...])
    to_genes(lambda peer: r_tot.at[1, gene], r_tot.at[1, gene], 8)
    r_sq[gene] = square_row(v1[...])
    to_genes(lambda peer: r_sq.at[gene], r_sq.at[gene], 9)
    counts_by_genes(v1[...])
    bmat = expo_by_genes(v1[...])

    wait_bytes(r_tot.at[1, pl.ds(0, N_GENE - 1)], recv_sem.at[8])
    size = lib[...] / jnp.sum(r_tot[1], axis=0)
    loadings_parts(1, u1[...], size)
    scatter_loadings(1, 10)
    r_vx[1, cell] = pv[1, cell]

    factor_parts(1, bmat, size)
    to_genes(lambda peer: pu.at[1, peer], r_ux.at[1, gene], 12)
    r_ux[1, gene] = pu[1, gene]

    shift = jnp.broadcast_to(jnp.log(size), (LANES, CELLS)).T
    for t in range(COLS):
        rate_v[:, t * LANES : (t + 1) * LANES] = (lin[:, t * LANES : (t + 1) * LANES] + shift).astype(BF16)
    out_r = pltpu.make_async_copy(rate_v, rate_o, out_sem.at[4])
    out_r.start()

    wait_bytes(r_ux.at[1, pl.ds(0, N_GENE - 1)], recv_sem.at[12])
    u_tile = u1[pl.ds(urow, 8), pl.ds(ucol, LANES)]
    grad = jnp.sum(r_ux[1], axis=0) - u_tile
    r_mu[gene] = mu_keep[...] + 0.5 * ustep * grad
    to_genes(lambda peer: r_mu.at[gene], r_mu.at[gene], 13)

    wait_bytes(r_sq.at[pl.ds(0, N_GENE - 1)], recv_sem.at[9])
    squares2 = jnp.sum(r_sq[...], axis=0)

    def second_update(tile, arrived, keep):
        b, where = v_tile_of(tile)
        vs = step_col(b)
        ard = genes_total / (col_of(squares2, b) + 2.0)
        r_mv[tile] = mv_keep[keep] + 0.5 * vs * (jnp.sum(arrived, axis=0) - ard * v1[where])

    arrived_parts(1, 10)
    second_update(cell, r_vx[1], 0)

    @pl.when(owns_extra)
    def _():
        second_update(N_CELL + cy, r_ve[1], 1)

    gather_loadings(r_mv, 14)

    wait_bytes(r_mu.at[pl.ds(0, N_GENE - 1)], recv_sem.at[13])
    for b in range(K // 8):
        for t in range(UCOLS):
            pfin[8 * b : 8 * b + 8, t * LANES : (t + 1) * LANES] = r_mu[b * UCOLS + t]
    out_p = pltpu.make_async_copy(pfin, p_o, out_sem.at[2])
    out_p.start()

    wait_bytes(r_tot.at[0, pl.ds(0, N_GENE - 1)], send_sem.at[0])
    wait_bytes(r_ls.at[pl.ds(0, N_GENE - 1)], send_sem.at[1])
    scatter_sent(0, 2)
    wait_bytes(r_ux.at[0, pl.ds(0, N_GENE - 1)], send_sem.at[4])
    wait_bytes(r_ua.at[pl.ds(0, N_GENE - 1)], send_sem.at[5])
    gather_sent(r_va, 6)
    wait_bytes(r_tot.at[1, pl.ds(0, N_GENE - 1)], send_sem.at[8])
    wait_bytes(r_sq.at[pl.ds(0, N_GENE - 1)], send_sem.at[9])
    scatter_sent(1, 10)
    wait_bytes(r_ux.at[1, pl.ds(0, N_GENE - 1)], send_sem.at[12])
    wait_bytes(r_mu.at[pl.ds(0, N_GENE - 1)], send_sem.at[13])

    gather_arrived(r_mv, 14)
    for b in range(K // 8):
        for t in range(COLS):
            qfin[8 * b : 8 * b + 8, t * LANES : (t + 1) * LANES] = r_mv[b * COLS + t]
    out_q = pltpu.make_async_copy(qfin, q_o, out_sem.at[3])
    out_q.start()
    gather_sent(r_mv, 14)
    for copy in (out_u, out_v, out_r, out_p, out_q):
        copy.wait()


def local(counts, cell_factors, loadings, cell_momenta, loading_momenta, step):
    padded = jnp.pad(step, (0, LANES - K)).reshape(1, LANES)
    vm = pltpu.VMEM
    scratch = [
        vm((CELLS, GENES), jnp.int32), vm((K, CELLS), F32), vm((K, GENES), F32), vm((K, CELLS), F32), vm((K, GENES), F32), vm((1, LANES), F32),
        vm((CELLS, GENES), BF16), vm((CELLS, GENES), F32), vm((CELLS, GENES), BF16), vm((CELLS, GENES), BF16),
        vm((CELLS, LANES), F32), vm((1, CELLS), F32), vm((K, CELLS), F32), vm((K, GENES), F32),
        vm((2, N_GENE, 1, CELLS), F32), vm((N_GENE, 1, CELLS + LANES), F32), vm((N_GENE, 1, LANES), F32),
        vm((2, U_TILES, 8, LANES), F32), vm((2, N_GENE, 8, LANES), F32), vm((U_TILES, 8, LANES), F32), vm((U_TILES, 8, LANES), F32),
        vm((2, V_TILES, 8, LANES), F32), vm((2, N_CELL, 8, LANES), F32), vm((2, N_CELL, 8, LANES), F32),
        vm((V_TILES, 8, LANES), F32), vm((V_TILES, 8, LANES), F32), vm((2, 8, LANES), F32), vm((8, LANES), F32),
        vm((K, CELLS), F32), vm((K, GENES), F32), vm((K, CELLS), F32), vm((K, GENES), F32), vm((CELLS, GENES), BF16),
        pltpu.SemaphoreType.DMA((6,)), pltpu.SemaphoreType.DMA((5,)),
        pltpu.SemaphoreType.DMA((16,)), pltpu.SemaphoreType.DMA((16,)), pltpu.SemaphoreType.REGULAR,
    ]
    return pl.pallas_call(
        kernel,
        out_shape=(
            jax.ShapeDtypeStruct((K, CELLS), F32),
            jax.ShapeDtypeStruct((K, GENES), F32),
            jax.ShapeDtypeStruct((K, CELLS), F32),
            jax.ShapeDtypeStruct((K, GENES), F32),
            jax.ShapeDtypeStruct((CELLS, GENES), BF16),
        ),
        in_specs=[pl.BlockSpec(memory_space=pl.ANY)] * 6,
        out_specs=[pl.BlockSpec(memory_space=pl.ANY)] * 5,
        scratch_shapes=scratch,
        compiler_params=pltpu.CompilerParams(collective_id=0, has_side_effects=True, vmem_limit_bytes=48 * 1024 * 1024),
    )(counts, cell_factors, loadings, cell_momenta, loading_momenta, padded)


def solution(mesh):
    placed = (
        P("cell", "gene"),
        P(None, "cell"),
        P(None, "gene"),
        P(None, "cell"),
        P(None, "gene"),
        P(),
    )
    return jax.shard_map(
        local,
        mesh=mesh,
        in_specs=placed,
        out_specs=(
            P(None, "cell"),
            P(None, "gene"),
            P(None, "cell"),
            P(None, "gene"),
            P("cell", "gene"),
        ),
        check_vma=False,
    )
```

time: 145 us -> 64.6 us (0.45)
  Pallas kernels: 0 us -> 55.1 us
  waiting for transfers between devices: 39.8 us -> 0 us
  starting transfers between devices: 38.6 us -> 0 us
  blocking collectives: 26.4 us -> 0 us
  between operations: 14.4 us -> 0.65 us
  other arithmetic: 10.3 us -> 0 us
  matrix products: 6.04 us -> 0 us
    pallas_call x0 -> x1, Pallas kernels: none -> 55.1 us  [local(): pl.pallas_call(kernel, out_shape=(jax.ShapeDtypeStruct((K, CELLS), F32),...]
    all_to_all x5 -> x0, waiting for transfers between devices: 39.4 us -> none  [the longest x3 21.1 us: from_everyone(): return lax.all_to_all(copies, axis, split_axis=0, concat_axis=0, tiled=True)]
    all_to_all x5 -> x0, starting transfers between devices: 38.6 us -> none  [the longest x3 20.6 us: from_everyone(): return lax.all_to_all(copies, axis, split_axis=0, concat_axis=0, tiled=True)]
    all_to_all x2 -> x0, blocking collectives: 26.4 us -> none  [from_everyone(): return lax.all_to_all(copies, axis, split_axis=0, concat_axis=0, tiled=True)]
    dot_general x6 -> x0, matrix products: 6.04 us -> none  [the longest x2 2.98 us: gradient(): lax.dot_general(loads, resid, (((1,), (1,)), ((), ())), precision=lax.Pre...]
    reduce_sum x10 -> x0, other arithmetic: 4.32 us -> none  [the longest x2 2.61 us: over_pieces(): return parts.sum(axis=0)]
    all_to_all x4 -> x0, other arithmetic: 4.28 us -> none  [the longest x2 2.14 us: from_everyone(): return lax.all_to_all(copies, axis, split_axis=0, concat_axis=0, tiled=True)]
    unnamed x30 -> x15, local copies, waits for them, and re-layouts: 5.22 us -> 7.91 us
  transfers between devices with their start and end apart: 7 -> 0, of which waited for: 6 -> 0; matrix products, arithmetic and copies ran while one was open for 10% -> 0% of each run, Pallas kernels for 0% -> 0%
where the time goes in v1:
time: 64.6 us; the launch traced here: 64.3 us
  Pallas kernels  55.1 us (85%)
  local copies, waits for them, and re-layouts  8.57 us (13%)
  between operations  0.65 us (1%)
    pallas_call x1, Pallas kernels, local(): pl.pallas_call(kernel, out_shape=(jax.ShapeDtypeStruct((K, CELLS), F32),...  55.1 us
    unnamed x15, local copies, waits for them, and re-layouts  7.91 us

profile of v1, /device:TPU:1, one launch (start us, length us, event | category | flops | bytes accessed | tf_op | source)
XLA Modules:
  0.0 64.3 jit_solution(5177602734910735070)
XLA Ops:
  0.6 0.7 %pad_bitcast_fusion.step_h = f32[1,128]{1,0:T(1,128)S(1)} fusion(f32[64]{0:T(128)} %param.11), kind=kLoop, calls=%fused_computation | loop fusion | bytes 768 | tf_op jit(solution)/shard_map/reshape | solution.py:434
  1.3 0.0 copy-start
  1.3 1.1 %copy-done = s32[256,640]{1,0:T(8,128)S(1)} copy-done((s32[256,640]{1,0:T(8,128)S(1)}, s32[256,640]{1,0:T(8,128)}, u32[]{:S(2)}) %copy-start) | copy-done | bytes 655384
  2.4 0.0 copy-start.1
  2.4 0.9 %copy-done.1 = f32[64,640]{1,0:T(8,128)S(1)} copy-done((f32[64,640]{1,0:T(8,128)S(1)}, f32[64,640]{1,0:T(8,128)}, u32[]{:S(2)}) %copy-start.1) | copy-done | bytes 163864
  3.3 0.0 copy-start.2
  3.3 0.9 %copy-done.2 = f32[64,640]{1,0:T(8,128)S(1)} copy-done((f32[64,640]{1,0:T(8,128)S(1)}, f32[64,640]{1,0:T(8,128)}, u32[]{:S(2)}) %copy-start.2) | copy-done | bytes 163864
  4.2 0.0 copy-start.3
  4.2 0.8 %copy-done.3 = f32[64,256]{1,0:T(8,128)S(1)} copy-done((f32[64,256]{1,0:T(8,128)S(1)}, f32[64,256]{1,0:T(8,128)}, u32[]{:S(2)}) %copy-start.3) | copy-done | bytes 65560
  5.1 0.0 copy-start.4
  5.1 0.8 %copy-done.4 = f32[64,256]{1,0:T(8,128)S(1)} copy-done((f32[64,256]{1,0:T(8,128)S(1)}, f32[64,256]{1,0:T(8,128)}, u32[]{:S(2)}) %copy-start.4) | copy-done | bytes 65560
  5.9 55.1 %shard_map.101 = (f32[64,256]{1,0:T(8,128)S(1)}, f32[64,640]{1,0:T(8,128)S(1)}, f32[64,256]{1,0:T(8,128)S(1)}, f32[64,640]{1,0:T(8,128)S(1)}, bf16[256,640]{1,0:T(8,128)(2,1)S(1)}) custom-call(s32[256,640]{1,0:T(8,128)S(1)} %copy-done, f32[64,256]{1,0:T(8,128)S(1)} %copy-done.3, f32[64,640]{1,0:T(8,128)S(1)} %copy-done.1, f32[64,256]{1,0:T(8,128)S(1)} %copy-done.4, ...), custom_call_target="tpu_custom_call" | custom-call | tf_op jit(solution)/shard_map/pallas_call | solution.py:448
  61.0 0.6 copy.16
  61.6 0.7 %copy.17 = f32[64,640]{1,0:T(8,128)} copy(f32[64,640]{1,0:T(8,128)S(1)} %get-tuple-element.11) | data formatting | bytes 327680
  62.3 0.6 copy.18
  62.9 0.7 %copy.19 = f32[64,640]{1,0:T(8,128)} copy(f32[64,640]{1,0:T(8,128)S(1)} %get-tuple-element.13) | data formatting | bytes 327680
  63.5 0.7 %copy.20 = bf16[256,640]{1,0:T(8,128)(2,1)} copy(bf16[256,640]{1,0:T(8,128)(2,1)S(1)} %get-tuple-element.14) | data formatting | bytes 655360
Async XLA Ops:
  1.3 1.1 %copy-start = (s32[256,640]{1,0:T(8,128)S(1)}, s32[256,640]{1,0:T(8,128)}, u32[]{:S(2)}) copy-start(s32[256,640]{1,0:T(8,128)} %counts_h.1) | copy-start | bytes 1966084
  2.4 0.9 %copy-start.1 = (f32[64,640]{1,0:T(8,128)S(1)}, f32[64,640]{1,0:T(8,128)}, u32[]{:S(2)}) copy-start(f32[64,640]{1,0:T(8,128)} %v_h.1) | copy-start | bytes 491524
  3.3 0.9 %copy-start.2 = (f32[64,640]{1,0:T(8,128)S(1)}, f32[64,640]{1,0:T(8,128)}, u32[]{:S(2)}) copy-start(f32[64,640]{1,0:T(8,128)} %q_h.1) | copy-start | bytes 491524
  4.2 0.8 %copy-start.3 = (f32[64,256]{1,0:T(8,128)S(1)}, f32[64,256]{1,0:T(8,128)}, u32[]{:S(2)}) copy-start(f32[64,256]{1,0:T(8,128)} %u_h.1) | copy-start | bytes 196612
  5.1 0.8 %copy-start.4 = (f32[64,256]{1,0:T(8,128)S(1)}, f32[64,256]{1,0:T(8,128)}, u32[]{:S(2)}) copy-start(f32[64,256]{1,0:T(8,128)} %p_h.1) | copy-start | bytes 196612

commit v2 on v1

--- a/solution.py
+++ b/solution.py
@@ -38,9 +38,8 @@
     return high, (x - high.astype(F32)).astype(BF16)
 
 
-def zigzag(i, n):
-    sign = 1 - 2 * rem(i, 2)
-    return n // 2 + sign * div(i + 1, 2)
+def far_first(n):
+    return sorted(range(n), key=lambda d: -min(d, n - d))
 
 
 def tiles_sum(x):
@@ -55,61 +54,44 @@
 
 
 def col_of(row, block):
-    lanes = lax.broadcasted_iota(jnp.int32, (8, LANES), 1)
-    wanted = lax.broadcasted_iota(jnp.int32, (8, LANES), 0) + 8 * block
-    return jnp.sum(jnp.where(lanes == wanted, jnp.broadcast_to(row, (8, LANES)), 0.0), axis=1, keepdims=True)
+    shape = (8, row.shape[1])
+    lanes = lax.broadcasted_iota(jnp.int32, shape, 1)
+    wanted = lax.broadcasted_iota(jnp.int32, shape, 0) + 8 * block
+    return jnp.sum(jnp.where(lanes == wanted, jnp.broadcast_to(row, shape), 0.0), axis=1, keepdims=True)
 
 
 def kernel(
     counts_h, u_h, v_h, p_h, q_h, step_h,
-    u_o, v_o, p_o, q_o, rate_o,
+    u1, v1, pfin, qfin, rate_v,
     cnt, u0, v0, p0, q0, stp,
     y16, lin, eh, el, part, lib, amat, cmat,
     r_tot, r_ls, r_sq, pu, r_ux, r_ua, r_mu, pv, r_vx, r_ve, r_va, r_mv, mv_keep, mu_keep,
-    u1, v1, pfin, qfin, rate_v,
-    in_sem, out_sem, send_sem, recv_sem, row_sem,
+    in_sem, send_sem, recv_sem, row_sem,
 ):
     cell = lax.axis_index("cell")
     gene = lax.axis_index("gene")
     cx, cy = div(cell, YS), rem(cell, YS)
     gz, gc = div(gene, CORES), rem(gene, CORES)
-    owns_extra = rem(cy, XS) == cx
+    owns_extra = rem(cy + 2 * gc, XS) == cx
+
+    xs = [rem(cx + d, XS) * YS for d in range(XS)]
+    ys = [rem(cy + d, YS) for d in range(YS)]
+    zs = [rem(gz + d, ZS) * CORES for d in range(ZS)]
+    cs = [gc, 1 - gc]
+    gene_peers = [zs[d] + cs[c] for d in far_first(ZS) for c in (1, 0) if (d, c) != (0, 0)]
+
+    barrier = pltpu.get_barrier_semaphore()
+    for peer in gene_peers:
+        pl.semaphore_signal(barrier, inc=1, device_id={"gene": peer}, device_id_type=MESH)
+    for d in far_first(YS)[:-1]:
+        pl.semaphore_signal(barrier, inc=1, device_id={"cell": xs[0] + ys[d]}, device_id_type=MESH)
+    for d in far_first(XS)[:-1]:
+        pl.semaphore_signal(barrier, inc=1, device_id={"cell": xs[d] + cy}, device_id_type=MESH)
 
     loads = {}
     for n, (src, dst) in enumerate(((u_h, u0), (v_h, v0), (counts_h, cnt), (q_h, q0), (step_h, stp), (p_h, p0))):
         loads[n] = pltpu.make_async_copy(src, dst, in_sem.at[n])
         loads[n].start()
-
-    def gene_peer(s):
-        i = div(s, 2)
-        zz = rem(gz + zigzag(i, ZS), ZS)
-        cc = rem(gc + 1 - rem(s, 2), CORES)
-        return zz * CORES + cc
-
-    def cell_peer(s):
-        xx = rem(cx + zigzag(rem(s, XS), XS), XS)
-        yy = rem(cy + zigzag(div(s, XS), YS), YS)
-        return xx * YS + yy
-
-    barrier = pltpu.get_barrier_semaphore()
-
-    def greet_gene(s, c):
-        pl.semaphore_signal(barrier, inc=1, device_id={"gene": gene_peer(s)}, device_id_type=MESH)
-        return c
-
-    def greet_y(s, c):
-        yy = rem(cy + s, YS)
-        pl.semaphore_signal(barrier, inc=1, device_id={"cell": cx * YS + yy}, device_id_type=MESH)
-        return c
-
-    def greet_x(s, c):
-        xx = rem(cx + s, XS)
-        pl.semaphore_signal(barrier, inc=1, device_id={"cell": xx * YS + cy}, device_id_type=MESH)
-        return c
-
-    lax.fori_loop(0, N_GENE - 1, greet_gene, 0)
-    lax.fori_loop(1, YS, greet_y, 0)
-    lax.fori_loop(1, XS, greet_x, 0)
 
     def wait_bytes(ref, sem):
         pltpu.make_async_copy(ref, ref, sem).wait()
@@ -121,34 +103,35 @@
         ).start()
 
     def to_genes(src_of, dst, phase):
-        def body(s, c):
-            peer = gene_peer(s)
+        for peer in gene_peers:
             push(src_of(peer), dst, phase, {"gene": peer})
-            return c
-        lax.fori_loop(0, N_GENE - 1, body, 0)
 
     def scatter_loadings(g, phase):
-        def body(s, c):
-            peer = cell_peer(s)
-            push(pv.at[g, peer], r_vx.at[g, cell], phase, {"cell": peer})
-            px, py = div(peer, YS), rem(peer, YS)
-
-            @pl.when(rem(py, XS) == px)
-            def _():
-                push(pv.at[g, N_CELL + py], r_ve.at[g, cell], phase + 1, {"cell": peer})
-            return c
-        lax.fori_loop(0, N_CELL - 1, body, 0)
+        for dy in far_first(YS):
+            def extra(dy=dy):
+                owner = rem(ys[dy] + 2 * gc, XS) * YS + ys[dy]
+                push(pv.at[g, N_CELL + ys[dy]], r_ve.at[g, cell], phase + 1, {"cell": owner})
+            if dy == 0:
+                pl.when(jnp.logical_not(owns_extra))(extra)
+            else:
+                extra()
+            for dx in far_first(XS):
+                if (dx, dy) != (0, 0):
+                    peer = xs[dx] + ys[dy]
+                    push(pv.at[g, peer], r_vx.at[g, cell], phase, {"cell": peer})
 
     def gather_loadings(buf, phase):
-        def body(s, c):
-            peer = cell_peer(s)
-            push(buf.at[cell], buf.at[cell], phase, {"cell": peer})
-
-            @pl.when(owns_extra)
-            def _():
-                push(buf.at[N_CELL + cy], buf.at[N_CELL + cy], phase + 1, {"cell": peer})
-            return c
-        lax.fori_loop(0, N_CELL - 1, body, 0)
+        def sends(also_extra):
+            for dy in far_first(YS):
+                for dx in far_first(XS):
+                    if (dx, dy) != (0, 0):
+                        peer = xs[dx] + ys[dy]
+                        push(buf.at[cell], buf.at[cell], phase, {"cell": peer})
+                        if also_extra:
+                            push(buf.at[N_CELL + cy], buf.at[N_CELL + cy], phase + 1, {"cell": peer})
+
+        pl.when(owns_extra)(lambda: sends(True))
+        pl.when(jnp.logical_not(owns_extra))(lambda: sends(False))
 
     def scatter_sent(g, phase):
         wait_bytes(r_vx.at[g, pl.ds(0, N_CELL - 1)], send_sem.at[phase])
@@ -257,20 +240,13 @@
     y16[...] = yf.astype(BF16)
     part[...] = tiles_sum(yf)
     lib_own = row_of(part[...])
-    r_tot[0, gene] = tot
-    r_ls[gene] = jnp.concatenate([lib_own, square_row(v0[...])], axis=1)
+    r_ls[gene] = jnp.concatenate([tot, lib_own, square_row(v0[...])], axis=1)
 
     pl.semaphore_wait(barrier, (N_GENE - 1) + (YS - 1) + (XS - 1))
 
-    to_genes(lambda peer: r_tot.at[0, gene], r_tot.at[0, gene], 0)
-    to_genes(lambda peer: r_ls.at[gene], r_ls.at[gene], 1)
-
-    def tell_x(s, c):
-        xx = rem(cx + s, XS)
-        pl.semaphore_signal(row_sem, inc=1, device_id={"cell": xx * YS + cy}, device_id_type=MESH)
-        return c
-
-    lax.fori_loop(1, XS, tell_x, 0)
+    to_genes(lambda peer: r_ls.at[gene], r_ls.at[gene], 0)
+    for d in far_first(XS)[:-1]:
+        pl.semaphore_signal(row_sem, inc=1, device_id={"cell": xs[d] + cy}, device_id_type=MESH)
 
     counts_by_cells(u0[...])
     counts_by_genes(v0[...])
@@ -278,12 +254,11 @@
     for n in (3, 4, 5):
         loads[n].wait()
 
-    wait_bytes(r_tot.at[0, pl.ds(0, N_GENE - 1)], recv_sem.at[0])
-    wait_bytes(r_ls.at[pl.ds(0, N_GENE - 1)], recv_sem.at[1])
-    both = jnp.sum(r_ls[...], axis=0)
-    lib[...] = both[:, :CELLS]
-    squares = both[:, CELLS:]
-    size = lib[...] / jnp.sum(r_tot[0], axis=0)
+    wait_bytes(r_ls.at[pl.ds(0, N_GENE - 1)], recv_sem.at[0])
+    sums = jnp.sum(r_ls[...], axis=0)
+    lib[...] = sums[:, CELLS : 2 * CELLS]
+    squares = sums[:, 2 * CELLS :]
+    size = lib[...] / sums[:, :CELLS]
     loadings_parts(0, u0[...], size)
     pl.semaphore_wait(row_sem, XS - 1)
     scatter_loadings(0, 2)
@@ -298,13 +273,6 @@
     ustep = step_col(ub)
     u_tile = u0[pl.ds(urow, 8), pl.ds(ucol, LANES)]
     p_tile = p0[pl.ds(urow, 8), pl.ds(ucol, LANES)]
-    wait_bytes(r_ux.at[0, pl.ds(0, N_GENE - 1)], recv_sem.at[4])
-    grad = jnp.sum(r_ux[0], axis=0) - u_tile
-    p_tile = p_tile + 0.5 * ustep * grad
-    mu_keep[...] = p_tile
-    r_ua[gene] = u_tile + ustep * p_tile
-    to_genes(lambda peer: r_ua.at[gene], r_ua.at[gene], 5)
-
     def v_tile_of(tile):
         b, t = div(tile, COLS), rem(tile, COLS)
         row, col = pl.multiple_of(b * 8, 8), pl.multiple_of(t * LANES, LANES)
@@ -338,30 +306,33 @@
 
     gather_loadings(r_va, 6)
 
+    wait_bytes(r_ux.at[0, pl.ds(0, N_GENE - 1)], recv_sem.at[4])
+    grad = jnp.sum(r_ux[0], axis=0) - u_tile
+    p_tile = p_tile + 0.5 * ustep * grad
+    mu_keep[...] = p_tile
+    r_ua[gene] = u_tile + ustep * p_tile
+    to_genes(lambda peer: r_ua.at[gene], r_ua.at[gene], 5)
+
     wait_bytes(r_ua.at[pl.ds(0, N_GENE - 1)], recv_sem.at[5])
     for b in range(K // 8):
         for t in range(UCOLS):
             u1[8 * b : 8 * b + 8, t * LANES : (t + 1) * LANES] = r_ua[b * UCOLS + t]
-    out_u = pltpu.make_async_copy(u1, u_o, out_sem.at[0])
-    out_u.start()
     counts_by_cells(u1[...])
 
     gather_arrived(r_va, 6)
     for b in range(K // 8):
         for t in range(COLS):
             v1[8 * b : 8 * b + 8, t * LANES : (t + 1) * LANES] = r_va[b * COLS + t]
-    out_v = pltpu.make_async_copy(v1, v_o, out_sem.at[1])
-    out_v.start()
-
-    r_tot[1, gene] = exponentials(u1[...], v1[...])
-    to_genes(lambda peer: r_tot.at[1, gene], r_tot.at[1, gene], 8)
+
+    r_tot[gene] = exponentials(u1[...], v1[...])
+    to_genes(lambda peer: r_tot.at[gene], r_tot.at[gene], 8)
     r_sq[gene] = square_row(v1[...])
     to_genes(lambda peer: r_sq.at[gene], r_sq.at[gene], 9)
     counts_by_genes(v1[...])
     bmat = expo_by_genes(v1[...])
 
-    wait_bytes(r_tot.at[1, pl.ds(0, N_GENE - 1)], recv_sem.at[8])
-    size = lib[...] / jnp.sum(r_tot[1], axis=0)
+    wait_bytes(r_tot.at[pl.ds(0, N_GENE - 1)], recv_sem.at[8])
+    size = lib[...] / jnp.sum(r_tot[...], axis=0)
     loadings_parts(1, u1[...], size)
     scatter_loadings(1, 10)
     r_vx[1, cell] = pv[1, cell]
@@ -373,8 +344,24 @@
     shift = jnp.broadcast_to(jnp.log(size), (LANES, CELLS)).T
     for t in range(COLS):
         rate_v[:, t * LANES : (t + 1) * LANES] = (lin[:, t * LANES : (t + 1) * LANES] + shift).astype(BF16)
-    out_r = pltpu.make_async_copy(rate_v, rate_o, out_sem.at[4])
-    out_r.start()
+
+    wait_bytes(r_sq.at[pl.ds(0, N_GENE - 1)], recv_sem.at[9])
+    squares2 = jnp.sum(r_sq[...], axis=0)
+
+    def second_update(tile, arrived, keep):
+        b, where = v_tile_of(tile)
+        vs = step_col(b)
+        ard = genes_total / (col_of(squares2, b) + 2.0)
+        r_mv[tile] = mv_keep[keep] + 0.5 * vs * (jnp.sum(arrived, axis=0) - ard * v1[where])
+
+    arrived_parts(1, 10)
+    second_update(cell, r_vx[1], 0)
+
+    @pl.when(owns_extra)
+    def _():
+        second_update(N_CELL + cy, r_ve[1], 1)
+
+    gather_loadings(r_mv, 14)
 
     wait_bytes(r_ux.at[1, pl.ds(0, N_GENE - 1)], recv_sem.at[12])
     u_tile = u1[pl.ds(urow, 8), pl.ds(ucol, LANES)]
@@ -382,38 +369,17 @@
     r_mu[gene] = mu_keep[...] + 0.5 * ustep * grad
     to_genes(lambda peer: r_mu.at[gene], r_mu.at[gene], 13)
 
-    wait_bytes(r_sq.at[pl.ds(0, N_GENE - 1)], recv_sem.at[9])
-    squares2 = jnp.sum(r_sq[...], axis=0)
-
-    def second_update(tile, arrived, keep):
-        b, where = v_tile_of(tile)
-        vs = step_col(b)
-        ard = genes_total / (col_of(squares2, b) + 2.0)
-        r_mv[tile] = mv_keep[keep] + 0.5 * vs * (jnp.sum(arrived, axis=0) - ard * v1[where])
-
-    arrived_parts(1, 10)
-    second_update(cell, r_vx[1], 0)
-
-    @pl.when(owns_extra)
-    def _():
-        second_update(N_CELL + cy, r_ve[1], 1)
-
-    gather_loadings(r_mv, 14)
-
     wait_bytes(r_mu.at[pl.ds(0, N_GENE - 1)], recv_sem.at[13])
     for b in range(K // 8):
         for t in range(UCOLS):
             pfin[8 * b : 8 * b + 8, t * LANES : (t + 1) * LANES] = r_mu[b * UCOLS + t]
-    out_p = pltpu.make_async_copy(pfin, p_o, out_sem.at[2])
-    out_p.start()
-
-    wait_bytes(r_tot.at[0, pl.ds(0, N_GENE - 1)], send_sem.at[0])
-    wait_bytes(r_ls.at[pl.ds(0, N_GENE - 1)], send_sem.at[1])
+
+    wait_bytes(r_ls.at[pl.ds(0, N_GENE - 1)], send_sem.at[0])
     scatter_sent(0, 2)
     wait_bytes(r_ux.at[0, pl.ds(0, N_GENE - 1)], send_sem.at[4])
     wait_bytes(r_ua.at[pl.ds(0, N_GENE - 1)], send_sem.at[5])
     gather_sent(r_va, 6)
-    wait_bytes(r_tot.at[1, pl.ds(0, N_GENE - 1)], send_sem.at[8])
+    wait_bytes(r_tot.at[pl.ds(0, N_GENE - 1)], send_sem.at[8])
     wait_bytes(r_sq.at[pl.ds(0, N_GENE - 1)], send_sem.at[9])
     scatter_sent(1, 10)
     wait_bytes(r_ux.at[1, pl.ds(0, N_GENE - 1)], send_sem.at[12])
@@ -423,42 +389,55 @@
     for b in range(K // 8):
         for t in range(COLS):
             qfin[8 * b : 8 * b + 8, t * LANES : (t + 1) * LANES] = r_mv[b * COLS + t]
-    out_q = pltpu.make_async_copy(qfin, q_o, out_sem.at[3])
-    out_q.start()
     gather_sent(r_mv, 14)
-    for copy in (out_u, out_v, out_r, out_p, out_q):
+
+
+def write_out(*refs):
+    sem = refs[10]
+    copies = [pltpu.make_async_copy(refs[n], refs[5 + n], sem.at[n]) for n in range(5)]
+    for copy in copies:
+        copy.start()
+    for copy in copies:
         copy.wait()
 
 
 def local(counts, cell_factors, loadings, cell_momenta, loading_momenta, step):
-    padded = jnp.pad(step, (0, LANES - K)).reshape(1, LANES)
+    arrays = (counts, cell_factors, loadings, cell_momenta, loading_momenta, step.reshape(1, K))
     vm = pltpu.VMEM
     scratch = [
-        vm((CELLS, GENES), jnp.int32), vm((K, CELLS), F32), vm((K, GENES), F32), vm((K, CELLS), F32), vm((K, GENES), F32), vm((1, LANES), F32),
+        vm((CELLS, GENES), jnp.int32), vm((K, CELLS), F32), vm((K, GENES), F32), vm((K, CELLS), F32), vm((K, GENES), F32), vm((1, K), F32),
         vm((CELLS, GENES), BF16), vm((CELLS, GENES), F32), vm((CELLS, GENES), BF16), vm((CELLS, GENES), BF16),
         vm((CELLS, LANES), F32), vm((1, CELLS), F32), vm((K, CELLS), F32), vm((K, GENES), F32),
-        vm((2, N_GENE, 1, CELLS), F32), vm((N_GENE, 1, CELLS + LANES), F32), vm((N_GENE, 1, LANES), F32),
+        vm((N_GENE, 1, CELLS), F32), vm((N_GENE, 1, 2 * CELLS + LANES), F32), vm((N_GENE, 1, LANES), F32),
         vm((2, U_TILES, 8, LANES), F32), vm((2, N_GENE, 8, LANES), F32), vm((U_TILES, 8, LANES), F32), vm((U_TILES, 8, LANES), F32),
         vm((2, V_TILES, 8, LANES), F32), vm((2, N_CELL, 8, LANES), F32), vm((2, N_CELL, 8, LANES), F32),
         vm((V_TILES, 8, LANES), F32), vm((V_TILES, 8, LANES), F32), vm((2, 8, LANES), F32), vm((8, LANES), F32),
-        vm((K, CELLS), F32), vm((K, GENES), F32), vm((K, CELLS), F32), vm((K, GENES), F32), vm((CELLS, GENES), BF16),
-        pltpu.SemaphoreType.DMA((6,)), pltpu.SemaphoreType.DMA((5,)),
+        pltpu.SemaphoreType.DMA((6,)),
         pltpu.SemaphoreType.DMA((16,)), pltpu.SemaphoreType.DMA((16,)), pltpu.SemaphoreType.REGULAR,
     ]
-    return pl.pallas_call(
+    shapes = (
+        jax.ShapeDtypeStruct((K, CELLS), F32),
+        jax.ShapeDtypeStruct((K, GENES), F32),
+        jax.ShapeDtypeStruct((K, CELLS), F32),
+        jax.ShapeDtypeStruct((K, GENES), F32),
+        jax.ShapeDtypeStruct((CELLS, GENES), BF16),
+    )
+    results = pl.pallas_call(
         kernel,
-        out_shape=(
-            jax.ShapeDtypeStruct((K, CELLS), F32),
-            jax.ShapeDtypeStruct((K, GENES), F32),
-            jax.ShapeDtypeStruct((K, CELLS), F32),
-            jax.ShapeDtypeStruct((K, GENES), F32),
-            jax.ShapeDtypeStruct((CELLS, GENES), BF16),
-        ),
-        in_specs=[pl.BlockSpec(memory_space=pl.ANY)] * 6,
-        out_specs=[pl.BlockSpec(memory_space=pl.ANY)] * 5,
+        out_shape=shapes,
+        in_specs=[pl.BlockSpec(memory_space=pltpu.HBM)] * 6,
+        out_specs=[pl.BlockSpec(memory_space=pltpu.VMEM)] * 5,
         scratch_shapes=scratch,
         compiler_params=pltpu.CompilerParams(collective_id=0, has_side_effects=True, vmem_limit_bytes=48 * 1024 * 1024),
-    )(counts, cell_factors, loadings, cell_momenta, loading_momenta, padded)
+    )(*(pltpu.with_memory_space_constraint(a, pltpu.HBM) for a in arrays))
+    return pl.pallas_call(
+        write_out,
+        out_shape=shapes,
+        in_specs=[pl.BlockSpec(memory_space=pltpu.VMEM)] * 5,
+        out_specs=[pl.BlockSpec(memory_space=pltpu.HBM)] * 5,
+        scratch_shapes=[pltpu.SemaphoreType.DMA((5,))],
+        compiler_params=pltpu.CompilerParams(vmem_limit_bytes=4 * 1024 * 1024),
+    )(*results)
 
 
 def solution(mesh):

time: 64.6 us -> 53.3 us (0.83)
  local copies, waits for them, and re-layouts: 8.57 us -> 0 us
  Pallas kernels: 55.1 us -> 52.5 us
    unnamed x15 -> x0, local copies, waits for them, and re-layouts: 7.91 us -> none
    pallas_call x1 -> x2, Pallas kernels: 55.1 us -> 52.5 us  [the longest x1 51.6 us: local(): pl.pallas_call(kernel, out_shape=shapes, in_specs=[pl.BlockSpec(memory_sp...]
    reshape x1 -> x0, local copies, waits for them, and re-layouts: 0.66 us -> none  [local(): padded = jnp.pad(step, (0, LANES - K)).reshape(1, LANES)]
where the time goes in v2:
time: 53.3 us; the launch traced here: 53.2 us
  Pallas kernels  52.5 us (98%)
  between operations  0.64 us (1%)
    pallas_call x1, Pallas kernels, local(): pl.pallas_call(kernel, out_shape=shapes, in_specs=[pl.BlockSpec(memory_sp...  51.6 us

profile of v2, /device:TPU:1, one launch (start us, length us, event | category | flops | bytes accessed | tf_op | source)
XLA Modules:
  0.0 53.2 jit_solution(9777769029835119082)
XLA Ops:
  0.6 51.6 %shard_map.101 = (f32[64,256]{1,0:T(8,128)S(1)}, f32[64,640]{1,0:T(8,128)S(1)}, f32[64,256]{1,0:T(8,128)S(1)}, f32[64,640]{1,0:T(8,128)S(1)}, bf16[256,640]{1,0:T(8,128)(2,1)S(1)}) custom-call(s32[256,640]{1,0:T(8,128)} %counts_h.1, f32[64,256]{1,0:T(8,128)} %u_h.1, f32[64,640]{1,0:T(8,128)} %v_h.1, f32[64,256]{1,0:T(8,128)} %p_h.1, f32[64,640]{1,0:T(8,128)} %q_h.1, ...), custom_call_target="tpu_custom_call" | custom-call | tf_op jit(solution)/shard_map/pallas_call | solution.py:425
  52.3 0.9 %shard_map.102 = (f32[64,256]{1,0:T(8,128)}, f32[64,640]{1,0:T(8,128)}, f32[64,256]{1,0:T(8,128)}, f32[64,640]{1,0:T(8,128)}, bf16[256,640]{1,0:T(8,128)(2,1)}) custom-call(f32[64,256]{1,0:T(8,128)S(1)} %get-tuple-element.10.refs_0_, f32[64,640]{1,0:T(8,128)S(1)} %get-tuple-element.11.refs_1_, f32[64,256]{1,0:T(8,128)S(1)} %get-tuple-element.12.refs_2_, ...), custom_call_target="tpu_custom_call" | custom-call | tf_op jit(solution)/shard_map/pallas_call | solution.py:433

commit v3 on v2

--- a/solution.py
+++ b/solution.py
@@ -17,7 +17,7 @@
 N_GENE = ZS * CORES
 V_TILES = (K // 8) * (GENES // LANES)
 U_TILES = (K // 8) * (CELLS // LANES)
-EXTRA = V_TILES - N_CELL
+HALVES = 2 * (V_TILES - N_CELL)
 COLS = GENES // LANES
 UCOLS = CELLS // LANES
 MESH = pl.DeviceIdType.MESH
@@ -42,6 +42,11 @@
     return sorted(range(n), key=lambda d: -min(d, n - d))
 
 
+def plane_far_first():
+    every = [(dx, dy) for dy in far_first(YS) for dx in far_first(XS)]
+    return sorted(every, key=lambda d: -min(d[0], XS - d[0]) - min(d[1], YS - d[1]))
+
+
 def tiles_sum(x):
     total = x[:, 0:LANES]
     for t in range(1, x.shape[1] // LANES):
@@ -65,14 +70,16 @@
     u1, v1, pfin, qfin, rate_v,
     cnt, u0, v0, p0, q0, stp,
     y16, lin, eh, el, part, lib, amat, cmat,
-    r_tot, r_ls, r_sq, pu, r_ux, r_ua, r_mu, pv, r_vx, r_ve, r_va, r_mv, mv_keep, mu_keep,
+    r_tot, r_ls, r_sq, pu, r_ux, r_ua, r_mu, pv, pvx, r_vx, r_ve, r_va, r_vah, r_mv, r_mvh, mv_keep, mv_half, mu_keep,
     in_sem, send_sem, recv_sem, row_sem,
 ):
     cell = lax.axis_index("cell")
     gene = lax.axis_index("gene")
     cx, cy = div(cell, YS), rem(cell, YS)
     gz, gc = div(gene, CORES), rem(gene, CORES)
-    owns_extra = rem(cy + 2 * gc, XS) == cx
+    owns_extra = rem(cx + cy + gc, 2) == 0
+    my_half = div(rem(cx + 16 - cy - gc, XS), 2)
+    extra_slot = 2 * cy + my_half
 
     xs = [rem(cx + d, XS) * YS for d in range(XS)]
     ys = [rem(cy + d, YS) for d in range(YS)]
@@ -108,27 +115,30 @@
 
     def scatter_loadings(g, phase):
         for dy in far_first(YS):
-            def extra(dy=dy):
-                owner = rem(ys[dy] + 2 * gc, XS) * YS + ys[dy]
-                push(pv.at[g, N_CELL + ys[dy]], r_ve.at[g, cell], phase + 1, {"cell": owner})
-            if dy == 0:
-                pl.when(jnp.logical_not(owns_extra))(extra)
-            else:
-                extra()
+            for h in range(2):
+                owner = rem(ys[dy] + 2 * h + gc, XS) * YS + ys[dy]
+
+                def extra(dy=dy, h=h, owner=owner):
+                    push(pvx.at[g, 2 * ys[dy] + h], r_ve.at[g, cell], phase + 1, {"cell": owner})
+
+                if dy == 0:
+                    pl.when(owner != cell)(extra)
+                else:
+                    extra()
             for dx in far_first(XS):
                 if (dx, dy) != (0, 0):
                     peer = xs[dx] + ys[dy]
                     push(pv.at[g, peer], r_vx.at[g, cell], phase, {"cell": peer})
 
-    def gather_loadings(buf, phase):
+    def gather_loadings(buf, halves, phase):
         def sends(also_extra):
-            for dy in far_first(YS):
-                for dx in far_first(XS):
+            for dx, dy in plane_far_first():
+                if True:
                     if (dx, dy) != (0, 0):
                         peer = xs[dx] + ys[dy]
                         push(buf.at[cell], buf.at[cell], phase, {"cell": peer})
                         if also_extra:
-                            push(buf.at[N_CELL + cy], buf.at[N_CELL + cy], phase + 1, {"cell": peer})
+                            push(halves.at[extra_slot], halves.at[extra_slot], phase + 1, {"cell": peer})
 
         pl.when(owns_extra)(lambda: sends(True))
         pl.when(jnp.logical_not(owns_extra))(lambda: sends(False))
@@ -138,29 +148,43 @@
 
         @pl.when(owns_extra)
         def _():
-            wait_bytes(r_vx.at[g, pl.ds(0, EXTRA - 1)], send_sem.at[phase + 1])
+            wait_bytes(r_ve.at[g, pl.ds(0, HALVES - 1)], send_sem.at[phase + 1])
 
         @pl.when(jnp.logical_not(owns_extra))
         def _():
-            wait_bytes(r_vx.at[g, pl.ds(0, EXTRA)], send_sem.at[phase + 1])
-
-    def gather_sent(buf, phase):
-        wait_bytes(buf.at[pl.ds(0, N_CELL - 1)], send_sem.at[phase])
+            wait_bytes(r_ve.at[g, pl.ds(0, HALVES)], send_sem.at[phase + 1])
+
+    def gather_sent(phase):
+        wait_bytes(r_vx.at[0, pl.ds(0, N_CELL - 1)], send_sem.at[phase])
 
         @pl.when(owns_extra)
         def _():
-            wait_bytes(buf.at[pl.ds(0, N_CELL - 1)], send_sem.at[phase + 1])
-
-    def gather_arrived(buf, phase):
+            wait_bytes(r_ve.at[0, pl.ds(0, N_CELL - 1)], send_sem.at[phase + 1])
+
+    def gather_arrived(buf, halves, phase):
         wait_bytes(buf.at[pl.ds(0, N_CELL - 1)], recv_sem.at[phase])
 
         @pl.when(owns_extra)
         def _():
-            wait_bytes(buf.at[pl.ds(0, EXTRA - 1)], recv_sem.at[phase + 1])
+            wait_bytes(halves.at[pl.ds(0, HALVES - 1)], recv_sem.at[phase + 1])
 
         @pl.when(jnp.logical_not(owns_extra))
         def _():
-            wait_bytes(buf.at[pl.ds(0, EXTRA)], recv_sem.at[phase + 1])
+            wait_bytes(halves, recv_sem.at[phase + 1])
+
+    def put_together(out, buf, halves):
+        for b in range(K // 8):
+            for t in range(COLS):
+                n = b * COLS + t
+                cols = slice(t * LANES, (t + 1) * LANES)
+                if n < N_CELL:
+                    out[8 * b : 8 * b + 8, cols] = buf[n]
+                else:
+                    out[8 * b : 8 * b + 4, cols] = halves[2 * (n - N_CELL)]
+                    out[8 * b + 4 : 8 * b + 8, cols] = halves[2 * (n - N_CELL) + 1]
+
+    def half(x):
+        return jnp.where(my_half == 1, x[4:8], x[0:4])
 
     chunks = []
     at = 0
@@ -221,7 +245,13 @@
             piece = cmat[:, lo : lo + wide] - (across(both) + rest)
             for t in range(wide // LANES):
                 for b in range(K // 8):
-                    pv[g, b * COLS + lo // LANES + t] = piece[8 * b : 8 * b + 8, t * LANES : (t + 1) * LANES]
+                    n = b * COLS + lo // LANES + t
+                    one = piece[8 * b : 8 * b + 8, t * LANES : (t + 1) * LANES]
+                    if n < N_CELL:
+                        pv[g, n] = one
+                    else:
+                        pvx[g, 2 * (n - N_CELL)] = one[0:4]
+                        pvx[g, 2 * (n - N_CELL) + 1] = one[4:8]
 
     def factor_parts(g, bmat, size):
         cross = amat[...] - size * bmat
@@ -280,13 +310,13 @@
 
     genes_total = float(GENES * N_GENE) + 2.0
 
-    def first_update(tile, arrived, keep):
+    def first_update(tile, arrived):
         b, where = v_tile_of(tile)
         vs = step_col(b)
         ard = genes_total / (col_of(squares, b) + 2.0)
         v = v0[where]
         mom = q0[where] + 0.5 * vs * (jnp.sum(arrived, axis=0) - ard * v)
-        mv_keep[keep] = mom
+        mv_keep[...] = mom
         r_va[tile] = v + vs * mom
 
     def arrived_parts(g, phase):
@@ -294,17 +324,23 @@
 
         @pl.when(owns_extra)
         def _():
-            r_ve[g, cell] = pv[g, N_CELL + cy]
+            r_ve[g, cell] = pvx[g, extra_slot]
             wait_bytes(r_ve.at[g, pl.ds(0, N_CELL - 1)], recv_sem.at[phase + 1])
 
     arrived_parts(0, 2)
-    first_update(cell, r_vx[0], 0)
+    first_update(cell, r_vx[0])
 
     @pl.when(owns_extra)
     def _():
-        first_update(N_CELL + cy, r_ve[0], 1)
-
-    gather_loadings(r_va, 6)
+        b, where = v_tile_of(N_CELL + cy)
+        vs = half(step_col(b))
+        ard = half(genes_total / (col_of(squares, b) + 2.0))
+        v = half(v0[where])
+        mom = half(q0[where]) + 0.5 * vs * (jnp.sum(r_ve[0], axis=0) - ard * v)
+        mv_half[...] = mom
+        r_vah[extra_slot] = v + vs * mom
+
+    gather_loadings(r_va, r_vah, 6)
 
     wait_bytes(r_ux.at[0, pl.ds(0, N_GENE - 1)], recv_sem.at[4])
     grad = jnp.sum(r_ux[0], axis=0) - u_tile
@@ -319,10 +355,8 @@
             u1[8 * b : 8 * b + 8, t * LANES : (t + 1) * LANES] = r_ua[b * UCOLS + t]
     counts_by_cells(u1[...])
 
-    gather_arrived(r_va, 6)
-    for b in range(K // 8):
-        for t in range(COLS):
-            v1[8 * b : 8 * b + 8, t * LANES : (t + 1) * LANES] = r_va[b * COLS + t]
+    gather_arrived(r_va, r_vah, 6)
+    put_together(v1, r_va, r_vah)
 
     r_tot[gene] = exponentials(u1[...], v1[...])
     to_genes(lambda peer: r_tot.at[gene], r_tot.at[gene], 8)
@@ -348,20 +382,23 @@
     wait_bytes(r_sq.at[pl.ds(0, N_GENE - 1)], recv_sem.at[9])
     squares2 = jnp.sum(r_sq[...], axis=0)
 
-    def second_update(tile, arrived, keep):
+    def second_update(tile, arrived):
         b, where = v_tile_of(tile)
         vs = step_col(b)
         ard = genes_total / (col_of(squares2, b) + 2.0)
-        r_mv[tile] = mv_keep[keep] + 0.5 * vs * (jnp.sum(arrived, axis=0) - ard * v1[where])
+        r_mv[tile] = mv_keep[...] + 0.5 * vs * (jnp.sum(arrived, axis=0) - ard * v1[where])
 
     arrived_parts(1, 10)
-    second_update(cell, r_vx[1], 0)
+    second_update(cell, r_vx[1])
 
     @pl.when(owns_extra)
     def _():
-        second_update(N_CELL + cy, r_ve[1], 1)
-
-    gather_loadings(r_mv, 14)
+        b, where = v_tile_of(N_CELL + cy)
+        ard = half(genes_total / (col_of(squares2, b) + 2.0))
+        grad = jnp.sum(r_ve[1], axis=0) - ard * half(v1[where])
+        r_mvh[extra_slot] = mv_half[...] + 0.5 * half(step_col(b)) * grad
+
+    gather_loadings(r_mv, r_mvh, 14)
 
     wait_bytes(r_ux.at[1, pl.ds(0, N_GENE - 1)], recv_sem.at[12])
     u_tile = u1[pl.ds(urow, 8), pl.ds(ucol, LANES)]
@@ -378,18 +415,16 @@
     scatter_sent(0, 2)
     wait_bytes(r_ux.at[0, pl.ds(0, N_GENE - 1)], send_sem.at[4])
     wait_bytes(r_ua.at[pl.ds(0, N_GENE - 1)], send_sem.at[5])
-    gather_sent(r_va, 6)
+    gather_sent(6)
     wait_bytes(r_tot.at[pl.ds(0, N_GENE - 1)], send_sem.at[8])
     wait_bytes(r_sq.at[pl.ds(0, N_GENE - 1)], send_sem.at[9])
     scatter_sent(1, 10)
     wait_bytes(r_ux.at[1, pl.ds(0, N_GENE - 1)], send_sem.at[12])
     wait_bytes(r_mu.at[pl.ds(0, N_GENE - 1)], send_sem.at[13])
 
-    gather_arrived(r_mv, 14)
-    for b in range(K // 8):
-        for t in range(COLS):
-            qfin[8 * b : 8 * b + 8, t * LANES : (t + 1) * LANES] = r_mv[b * COLS + t]
-    gather_sent(r_mv, 14)
+    gather_arrived(r_mv, r_mvh, 14)
+    put_together(qfin, r_mv, r_mvh)
+    gather_sent(14)
 
 
 def write_out(*refs):
@@ -410,8 +445,8 @@
         vm((CELLS, LANES), F32), vm((1, CELLS), F32), vm((K, CELLS), F32), vm((K, GENES), F32),
         vm((N_GENE, 1, CELLS), F32), vm((N_GENE, 1, 2 * CELLS + LANES), F32), vm((N_GENE, 1, LANES), F32),
         vm((2, U_TILES, 8, LANES), F32), vm((2, N_GENE, 8, LANES), F32), vm((U_TILES, 8, LANES), F32), vm((U_TILES, 8, LANES), F32),
-        vm((2, V_TILES, 8, LANES), F32), vm((2, N_CELL, 8, LANES), F32), vm((2, N_CELL, 8, LANES), F32),
-        vm((V_TILES, 8, LANES), F32), vm((V_TILES, 8, LANES), F32), vm((2, 8, LANES), F32), vm((8, LANES), F32),
+        vm((2, N_CELL, 8, LANES), F32), vm((2, HALVES, 4, LANES), F32), vm((2, N_CELL, 8, LANES), F32), vm((2, N_CELL, 4, LANES), F32),
+        vm((N_CELL, 8, LANES), F32), vm((HALVES, 4, LANES), F32), vm((N_CELL, 8, LANES), F32), vm((HALVES, 4, LANES), F32), vm((8, LANES), F32), vm((4, LANES), F32), vm((8, LANES), F32),
         pltpu.SemaphoreType.DMA((6,)),
         pltpu.SemaphoreType.DMA((16,)), pltpu.SemaphoreType.DMA((16,)), pltpu.SemaphoreType.REGULAR,
     ]

time: 53.3 us -> 53.6 us (level)
  no operation moved by 1% of the time
where the time goes in v3:
time: 53.6 us; the launch traced here: 53.4 us
  Pallas kernels  52.8 us (99%)
  between operations  0.64 us (1%)
    pallas_call x1, Pallas kernels, local(): pl.pallas_call(kernel, out_shape=shapes, in_specs=[pl.BlockSpec(memory_sp...  51.9 us

profile of v3, /device:TPU:1, one launch (start us, length us, event | category | flops | bytes accessed | tf_op | source)
XLA Modules:
  0.0 53.4 jit_solution(11096569669815982960)
XLA Ops:
  0.6 51.9 %shard_map.101 = (f32[64,256]{1,0:T(8,128)S(1)}, f32[64,640]{1,0:T(8,128)S(1)}, f32[64,256]{1,0:T(8,128)S(1)}, f32[64,640]{1,0:T(8,128)S(1)}, bf16[256,640]{1,0:T(8,128)(2,1)S(1)}) custom-call(s32[256,640]{1,0:T(8,128)} %counts_h.1, f32[64,256]{1,0:T(8,128)} %u_h.1, f32[64,640]{1,0:T(8,128)} %v_h.1, f32[64,256]{1,0:T(8,128)} %p_h.1, f32[64,640]{1,0:T(8,128)} %q_h.1, ...), custom_call_target="tpu_custom_call" | custom-call | tf_op jit(solution)/shard_map/pallas_call | solution.py:460
  52.5 0.9 %shard_map.102 = (f32[64,256]{1,0:T(8,128)}, f32[64,640]{1,0:T(8,128)}, f32[64,256]{1,0:T(8,128)}, f32[64,640]{1,0:T(8,128)}, bf16[256,640]{1,0:T(8,128)(2,1)}) custom-call(f32[64,256]{1,0:T(8,128)S(1)} %get-tuple-element.10.refs_0_, f32[64,640]{1,0:T(8,128)S(1)} %get-tuple-element.11.refs_1_, f32[64,256]{1,0:T(8,128)S(1)} %get-tuple-element.12.refs_2_, ...), custom_call_target="tpu_custom_call" | custom-call | tf_op jit(solution)/shard_map/pallas_call | solution.py:468

commit v4 on v3

--- a/solution.py
+++ b/solution.py
@@ -69,7 +69,7 @@
     counts_h, u_h, v_h, p_h, q_h, step_h,
     u1, v1, pfin, qfin, rate_v,
     cnt, u0, v0, p0, q0, stp,
-    y16, lin, eh, el, part, lib, amat, cmat,
+    y16, lin, expo, eh, el, part, lib, amat, cmat,
     r_tot, r_ls, r_sq, pu, r_ux, r_ua, r_mu, pv, pvx, r_vx, r_ve, r_va, r_vah, r_mv, r_mvh, mv_keep, mv_half, mu_keep,
     in_sem, send_sem, recv_sem, row_sem,
 ):
@@ -114,21 +114,23 @@
             push(src_of(peer), dst, phase, {"gene": peer})
 
     def scatter_loadings(g, phase):
-        for dy in far_first(YS):
-            for h in range(2):
-                owner = rem(ys[dy] + 2 * h + gc, XS) * YS + ys[dy]
-
-                def extra(dy=dy, h=h, owner=owner):
-                    push(pvx.at[g, 2 * ys[dy] + h], r_ve.at[g, cell], phase + 1, {"cell": owner})
-
-                if dy == 0:
-                    pl.when(owner != cell)(extra)
-                else:
-                    extra()
-            for dx in far_first(XS):
-                if (dx, dy) != (0, 0):
-                    peer = xs[dx] + ys[dy]
-                    push(pv.at[g, peer], r_vx.at[g, cell], phase, {"cell": peer})
+        greeted = set()
+        for dx, dy in plane_far_first():
+            if dy not in greeted:
+                greeted.add(dy)
+                for h in range(2):
+                    owner = rem(ys[dy] + 2 * h + gc, XS) * YS + ys[dy]
+
+                    def extra(dy=dy, h=h, owner=owner):
+                        push(pvx.at[g, 2 * ys[dy] + h], r_ve.at[g, cell], phase + 1, {"cell": owner})
+
+                    if dy == 0:
+                        pl.when(owner != cell)(extra)
+                    else:
+                        extra()
+            if (dx, dy) != (0, 0):
+                peer = xs[dx] + ys[dy]
+                push(pv.at[g, peer], r_vx.at[g, cell], phase, {"cell": peer})
 
     def gather_loadings(buf, halves, phase):
         def sends(also_extra):
@@ -202,12 +204,16 @@
             x = jnp.dot(left, right[:, lo : lo + wide], preferred_element_type=F32)
             e = jnp.exp(x)
             lin[:, lo : lo + wide] = x
-            high, low = split(e)
-            eh[:, lo : lo + wide] = high
-            el[:, lo : lo + wide] = low
+            expo[:, lo : lo + wide] = e
             some = tiles_sum(e)
             part[...] = some if n == 0 else part[...] + some
         return row_of(part[...])
+
+    def in_halves():
+        for lo, wide in chunks:
+            high, low = split(expo[:, lo : lo + wide])
+            eh[:, lo : lo + wide] = high
+            el[:, lo : lo + wide] = low
 
     def square_row(v):
         s = tiles_sum(v * v)
@@ -278,6 +284,7 @@
     for d in far_first(XS)[:-1]:
         pl.semaphore_signal(row_sem, inc=1, device_id={"cell": xs[d] + cy}, device_id_type=MESH)
 
+    in_halves()
     counts_by_cells(u0[...])
     counts_by_genes(v0[...])
     bmat = expo_by_genes(v0[...])
@@ -362,6 +369,7 @@
     to_genes(lambda peer: r_tot.at[gene], r_tot.at[gene], 8)
     r_sq[gene] = square_row(v1[...])
     to_genes(lambda peer: r_sq.at[gene], r_sq.at[gene], 9)
+    in_halves()
     counts_by_genes(v1[...])
     bmat = expo_by_genes(v1[...])
 
@@ -441,7 +449,7 @@
     vm = pltpu.VMEM
     scratch = [
         vm((CELLS, GENES), jnp.int32), vm((K, CELLS), F32), vm((K, GENES), F32), vm((K, CELLS), F32), vm((K, GENES), F32), vm((1, K), F32),
-        vm((CELLS, GENES), BF16), vm((CELLS, GENES), F32), vm((CELLS, GENES), BF16), vm((CELLS, GENES), BF16),
+        vm((CELLS, GENES), BF16), vm((CELLS, GENES), F32), vm((CELLS, GENES), F32), vm((CELLS, GENES), BF16), vm((CELLS, GENES), BF16),
         vm((CELLS, LANES), F32), vm((1, CELLS), F32), vm((K, CELLS), F32), vm((K, GENES), F32),
         vm((N_GENE, 1, CELLS), F32), vm((N_GENE, 1, 2 * CELLS + LANES), F32), vm((N_GENE, 1, LANES), F32),
         vm((2, U_TILES, 8, LANES), F32), vm((2, N_GENE, 8, LANES), F32), vm((U_TILES, 8, LANES), F32), vm((U_TILES, 8, LANES), F32),

time: 53.6 us -> 53.2 us (level)
  no operation moved by 1% of the time
where the time goes in v4:
time: 53.2 us; the launch traced here: 53.1 us
  Pallas kernels  52.4 us (98%)
  between operations  0.64 us (1%)
    pallas_call x1, Pallas kernels, local(): pl.pallas_call(kernel, out_shape=shapes, in_specs=[pl.BlockSpec(memory_sp...  51.5 us

profile of v4, /device:TPU:1, one launch (start us, length us, event | category | flops | bytes accessed | tf_op | source)
XLA Modules:
  0.0 53.1 jit_solution(562387213737575083)
XLA Ops:
  0.6 51.5 %shard_map.101 = (f32[64,256]{1,0:T(8,128)S(1)}, f32[64,640]{1,0:T(8,128)S(1)}, f32[64,256]{1,0:T(8,128)S(1)}, f32[64,640]{1,0:T(8,128)S(1)}, bf16[256,640]{1,0:T(8,128)(2,1)S(1)}) custom-call(s32[256,640]{1,0:T(8,128)} %counts_h.1, f32[64,256]{1,0:T(8,128)} %u_h.1, f32[64,640]{1,0:T(8,128)} %v_h.1, f32[64,256]{1,0:T(8,128)} %p_h.1, f32[64,640]{1,0:T(8,128)} %q_h.1, ...), custom_call_target="tpu_custom_call" | custom-call | tf_op jit(solution)/shard_map/pallas_call | solution.py:468
  52.2 0.9 %shard_map.102 = (f32[64,256]{1,0:T(8,128)}, f32[64,640]{1,0:T(8,128)}, f32[64,256]{1,0:T(8,128)}, f32[64,640]{1,0:T(8,128)}, bf16[256,640]{1,0:T(8,128)(2,1)}) custom-call(f32[64,256]{1,0:T(8,128)S(1)} %get-tuple-element.10.refs_0_, f32[64,640]{1,0:T(8,128)S(1)} %get-tuple-element.11.refs_1_, f32[64,256]{1,0:T(8,128)S(1)} %get-tuple-element.12.refs_2_, ...), custom_call_target="tpu_custom_call" | custom-call | tf_op jit(solution)/shard_map/pallas_call | solution.py:476
